TPU v7x, 32 devices: a whole 2x2x4 slice. The times are simulated.
32 devices in a mesh: ctx: 8 (over y, x, core), tp: 4 (over z).
Axes of the slice: x: 2, y: 2, z: 4, core: 2. Of those that a mesh axis runs over, the one named last changes fastest.
Arguments:
- tokens: bfloat16 [4096, 768], P('ctx'), may hold values from -6 to 6
- cotangent: bfloat16 [4096, 768], P('ctx'), may hold values from -8 to 8
- block_pos: int32 [32], replicated, may hold values from 0 to 15, as said below
- block_seq: int32 [32], replicated, may hold values from 0 to 1, as said below
- ln1_gain: float32 [768], replicated, may hold values from 0.5 to 1.5
- ln1_bias: float32 [768], replicated, may hold values from -1.2 to 1.2
- qkv_weight: bfloat16 [768, 3, 768], P(None, None, 'tp'), may hold values from -5 to 5
- qv_bias: float32 [2, 768], P(None, 'tp'), may hold values from -2.5 to 2.5
- out_weight: bfloat16 [768, 768], P('tp'), may hold values from -6 to 6
- out_bias: float32 [768], replicated, may hold values from -1.2 to 1.2
- ln2_gain: float32 [768], replicated, may hold values from 0.5 to 1.5
- ln2_bias: float32 [768], replicated, may hold values from -1.2 to 1.2
- fc_weight: bfloat16 [768, 3072], P(None, 'tp'), may hold values from -0.4375 to 0.4375
- fc_bias: float32 [3072], P('tp'), may hold values from -2.5 to 2.5
- proj_weight: bfloat16 [3072, 768], P('tp'), may hold values from -0.21875 to 0.21875
- proj_bias: float32 [768], replicated, may hold values from -1.2 to 1.2
Outputs:
- output: bfloat16 [4096, 768], P('ctx')
- grad_tokens: bfloat16 [4096, 768], P('ctx')
- grad_ln1_gain: float32 [768], replicated
- grad_ln1_bias: float32 [768], replicated
- grad_qkv_weight: float32 [768, 3, 768], P(None, None, 'tp')
- grad_qv_bias: float32 [2, 768], P(None, 'tp')
- grad_out_weight: float32 [768, 768], P('tp')
- grad_out_bias: float32 [768], replicated
- grad_ln2_gain: float32 [768], replicated
- grad_ln2_bias: float32 [768], replicated
- grad_fc_weight: float32 [768, 3072], P(None, 'tp')
- grad_fc_bias: float32 [3072], P('tp')
- grad_proj_weight: float32 [3072, 768], P('tp')
- grad_proj_bias: float32 [768], replicated
Inputs may be any that keep to these rules, and one draw needn't show every extreme that they name: `block_pos`: block b holds tokens [b * 128, (b+1) * 128) of the whole; each index r of ctx holds blocks 4r to 4r+3, two of each sequence, at positions p and 15 - p; every position of each sequence is held by exactly one block. `block_seq`: two sequences; each index of ctx holds two blocks of each.
All inputs are finite; a program needn't handle non-finite values.
Results may differ from a plain program's by a relative error of at most 0.025.
Values may be sent and summed in bfloat16 or wider, within the bound.
A program may use at most 320 MiB of HBM per device.

v0:
```python
import functools
from types import SimpleNamespace

import jax
import jax.numpy as jnp
from jax import lax
from jax.experimental import pallas as pl
from jax.experimental.pallas import tpu as pltpu
from jax.sharding import PartitionSpec as P

HEAD = 64
BLK = 128
BF = jnp.bfloat16
F32 = jnp.float32
MESH = pl.DeviceIdType.MESH
NEG = -1e30
C0 = 0.7978845608028654
C1 = 0.044715


def dg(a, b, ca, cb):
    return lax.dot_general(a, b, (((ca,), (cb,)), ((), ())), preferred_element_type=F32)


def normed(x):
    centre = jnp.mean(x, axis=-1, keepdims=True)
    shifted = x - centre
    spread = jnp.mean(shifted * shifted, axis=-1, keepdims=True)
    inverse = lax.rsqrt(spread + 1e-05)
    return shifted * inverse, inverse


def fold8(x):
    rows, width = x.shape
    return jnp.sum(x.reshape(rows // 8, 8, width), axis=0)


def roll64(x):
    return pltpu.roll(x, 64, 1)


def scratch_list(R, T, D, F, nh):
    NG = R // 2
    N = 4 * BLK
    v = pltpu.VMEM
    out = [
        ("tok_raw", v((4, BLK, D), BF)),
        ("cot_raw", v((4, BLK, D), BF)),
        ("stage", v((2, 2, BLK, D), BF)),
        ("x", v((4, BLK, D), BF)),
        ("cot", v((4, BLK, D), BF)),
        ("wqt", v((640, D), BF)),
        ("wo", v((T, nh * HEAD, D), BF)),
        ("wolo", v((T, BLK, D), BF)),
        ("wohi", v((T, BLK, D), BF)),
        ("wopad", v((nh * BLK, D), BF)),
        ("fc", v((D, F), BF)),
        ("pw", v((F, D), BF)),
        ("brow", v((1, 640), F32)),
        ("act1", v((4, BLK, D), BF)),
        ("q", v((nh, N, 128), BF)),
        ("kv", v((NG, nh, N, 128), BF)),
        ("pre", v((N, D), F32)),
        ("ga", v((N, F), F32)),
        ("hid", v((N, D), F32)),
        ("act2", v((N, D), BF)),
        ("actd", v((N, F), BF)),
        ("gpre", v((N, F), BF)),
        ("mlo", v((256, 256), F32)),
        ("mhi", v((256, 256), F32)),
        ("m", v((2 * nh, 1, 256), F32)),
        ("l", v((2 * nh, 1, 256), F32)),
        ("delta", v((2 * nh, 1, 256), F32)),
        ("acc", v((2 * nh, 128, 256), F32)),
        ("attp", v((nh, N, 128), BF)),
        ("attn", v((N, 256), BF)),
        ("ab", v((T, 768, 128), BF)),
        ("p1", v((4, BLK, D), BF)),
        ("r1", v((4, BLK, D), BF)),
        ("l1", v((4, BLK, D), BF)),
        ("p2", v((4, BLK, D), BF)),
        ("r2", v((4, BLK, D), BF)),
        ("l2", v((4, BLK, D), BF)),
        ("p3", v((4, BLK, D), BF)),
        ("r3", v((4, BLK, D), BF)),
        ("l3", v((4, BLK, D), BF)),
        ("tot", v((BLK, D), F32)),
        ("gh", v((BLK, D), F32)),
        ("h", v((4, BLK, D), BF)),
        ("do", v((nh, N, 128), BF)),
        ("dk", v((NG, nh, N, 128), BF)),
        ("dkr", v((NG, nh, N, 128), BF)),
        ("dka", v((2, nh, 256, 128), BF)),
        ("gn", v((N, 640), BF)),
        ("gt", v((640, N), BF)),
        ("w1", v((2, NG, D // NG, D), BF)),
        ("w1r", v((NG, D // NG, D), BF)),
        ("w1s", v((NG, D // NG, D), BF)),
        ("w1f", v((2, NG, D // NG, D), BF)),
        ("w2", v((2, NG, D // 2 // NG, D), BF)),
        ("w2r", v((NG, D // 2 // NG, D), BF)),
        ("w2s", v((NG, D // 2 // NG, D), BF)),
        ("w2f", v((2, NG, D // 2 // NG, D), BF)),
        ("osh", v((BLK, D), BF)),
        ("gsh", v((BLK, D), BF)),
        ("fo", v((2, 2, BLK, D), BF)),
        ("fg", v((2, 2, BLK, D), BF)),
        ("vsum", v((16, D), F32)),
        ("vz", v((T, 16, D), BF)),
        ("vc", v((R, 16, D), BF)),
        ("ss", pltpu.SemaphoreType.DMA((96 + 16 * NG,))),
        ("rs", pltpu.SemaphoreType.DMA((96 + 16 * NG,))),
        ("ls", pltpu.SemaphoreType.DMA((16,))),
    ]
    return out


def layer_kernel(R, T, D, F, nh, names, *refs):
    (pos_ref, seq_ref, tok_hbm, cot_hbm, g1_ref, b1_ref, wqt_hbm, qvb_ref, wo_hbm, ob_ref, g2_ref,
     b2_ref, fc_hbm, fcb_ref, pw_hbm, pb_ref, w1_out, w2_out, fo_out, fg_out, v_out) = refs[:21]
    s = SimpleNamespace(**dict(zip(names, refs[21:])))
    NG = R // 2
    N = 4 * BLK
    Q1 = D // NG
    Q2 = D // 2 // NG
    r = lax.axis_index("ctx")
    z = lax.axis_index("tp")
    c = lax.rem(r, 2)
    o = 1 - c
    g = lax.div(r, 2)
    mate = 2 * g + o
    if NG == 4:
        ga_ = g + 1 - 2 * lax.rem(g, 2)
        gb_ = g + 2 - 4 * lax.div(g, 2)
        gc_ = ga_ + 2 - 4 * lax.div(ga_, 2)
        peers = [g, ga_, gb_, gc_]
        sources = peers
    else:
        peers = [lax.rem(g + t, NG) for t in range(NG)]
        sources = [lax.rem(g + NG - t, NG) for t in range(NG)]

    pending = []
    ids = [0]

    def new(count=1):
        first = ids[0]
        ids[0] += count
        assert ids[0] <= 96 + 16 * NG
        return first

    def remote(src, dst, slot, dev):
        return pltpu.make_async_remote_copy(
            src_ref=src, dst_ref=dst, send_sem=s.ss.at[slot], recv_sem=s.rs.at[slot],
            device_id=dev, device_id_type=MESH)

    def send(src, dst, slot, dev, cond=None):
        def go():
            remote(src, dst, slot, dev).start()

        def done():
            remote(src, dst, slot, dev).wait_send()

        if cond is None:
            go()
        else:
            pl.when(cond)(go)
        pending.append((cond, done))

    def arrived(dst, slot, cond=None):
        def go():
            remote(dst, dst, slot, (r, z)).wait_recv()

        if cond is None:
            go()
        else:
            pl.when(cond)(go)

    loads = {}

    def load(name, src, dst, k):
        loads[name] = pltpu.make_async_copy(src, dst, s.ls.at[k])
        loads[name].start()

    load("tok", tok_hbm, s.tok_raw, 0)
    load("wqt", wqt_hbm, s.wqt.at[pl.ds(0, 3 * nh * HEAD)], 1)
    load("cot", cot_hbm, s.cot_raw, 2)
    load("wo", wo_hbm, s.wo.at[z], 3)
    load("pw", pw_hbm, s.pw, 4)
    load("fc", fc_hbm, s.fc, 5)

    barrier = pltpu.get_barrier_semaphore()
    for t in range(1, R):
        pl.semaphore_signal(barrier, inc=1, device_id=(lax.rem(r + t, R), z), device_id_type=MESH)
    for t in range(1, T):
        pl.semaphore_signal(barrier, inc=1, device_id=(r, lax.rem(z + t, T)), device_id_type=MESH)
    pl.semaphore_wait(barrier, R - 1 + T - 1)

    def find(seq):
        low = jnp.int32(0)
        high = jnp.int32(0)
        for b in range(4):
            same = seq_ref[4 * r + b] == seq
            first = pos_ref[4 * r + b] < R
            low = jnp.where(same & first, b, low)
            high = jnp.where(same & jnp.logical_not(first), b, high)
        return low, high

    def low_pos(rank):
        total = jnp.int32(0)
        for b in range(4):
            here = (seq_ref[4 * rank + b] == c) & (pos_ref[4 * rank + b] < R)
            total = total + jnp.where(here, pos_ref[4 * rank + b], 0)
        return total

    other = find(o)
    own = find(c)
    q_low = (low_pos(2 * g), low_pos(2 * g + 1))

    sx = new(4)
    loads["tok"].wait()
    for k in range(2):
        s.stage[0, k] = s.tok_raw[other[k]]
        send(s.stage.at[0, k], s.x.at[2 * k + c], sx + k, (mate, z))
    for k in range(2):
        s.x[2 * k + c] = s.tok_raw[own[k]]
    loads["wo"].wait()

    def line_send(buf, at, base, right, left):
        if right is not None:
            send(buf.at[at], buf.at[at], base + right[1], (r, z + 1), right[0])
        if left is not None:
            send(buf.at[at], buf.at[at], base + left[1], (r, z - 1), left[0])

    class Line:
        def __init__(self, buf):
            self.buf = buf
            self.base = new(2 * (T - 1))

        def start(self):
            send(self.buf.at[z], self.buf.at[z], self.base, (r, z + 1), z < T - 1)
            send(self.buf.at[z], self.buf.at[z], self.base + T - 1, (r, z - 1), z > 0)

        def step(self, k):
            left_src = jnp.maximum(z - k, 0)
            right_src = jnp.minimum(z + k, T - 1)
            arrived(self.buf.at[left_src], self.base + k - 1, z >= k)
            if k < T - 1:
                send(self.buf.at[left_src], self.buf.at[left_src], self.base + k, (r, z + 1),
                     (z >= k) & (z < T - 1))
            arrived(self.buf.at[right_src], self.base + T - 1 + k - 1, z <= T - 1 - k)
            if k < T - 1:
                send(self.buf.at[right_src], self.buf.at[right_src], self.base + T - 1 + k,
                     (r, z - 1), (z <= T - 1 - k) & (z > 0))

    class Fold:
        def __init__(self, part, from_left, from_right):
            self.part, self.fl, self.fr = part, from_left, from_right
            self.base = new(2 * T)

        def _one(self, d, buf, slot, to, inner, more):
            def both():
                arrived(buf.at[d], slot)

            pl.when(inner & (more | (z == d)))(both)

            def add():
                self.part[d] = (self.part[d].astype(F32) + buf[d].astype(F32)).astype(BF)

            pl.when(inner & more)(add)
            send(self.part.at[d], buf.at[d], slot, (r, to), inner & more)

        def begin_right(self, d):
            send(self.part.at[d], self.fl.at[d], self.base + d, (r, z + 1), z == 0)

        def begin_left(self, d):
            send(self.part.at[d], self.fr.at[d], self.base + T + d, (r, z - 1), z == T - 1)

        def step(self, j):
            d = T - 1 - j
            self._one(d, self.fl, self.base + d, z + 1, z > 0, z < d)
            self._one(j, self.fr, self.base + T + j, z - 1, z < T - 1, z > j)

        def total(self):
            s.tot[...] = self.part[z].astype(F32)

            @pl.when(z > 0)
            def _():
                s.tot[...] += self.fl[z].astype(F32)

            @pl.when(z < T - 1)
            def _():
                s.tot[...] += self.fr[z].astype(F32)

    class Spread:
        def __init__(self, shard, out):
            self.shard, self.out = shard, out
            self.base = new(9)
            self.half = lax.div(z, 2)
            self.par = lax.rem(z, 2)

        def start(self):
            @pl.when(self.par == c)
            def _():
                self.out[self.half, c] = self.shard[...]

            send(self.shard, self.out.at[self.half, c], self.base + 8, (mate, z), self.par != c)
            for k in range(2):
                self._go(k, 0, z == c + 2 * k)

        def _go(self, k, item, cond):
            src = c + 2 * k
            q = c if item == 0 else o
            blk = self.out.at[k, q]
            send(blk, blk, self.base + 2 * k + item, (r, z + 1), cond & (z >= src) & (z < T - 1))
            send(blk, blk, self.base + 4 + 2 * k + item, (r, z - 1), cond & (z <= src) & (z > 0))

        def swapped(self):
            arrived(self.out.at[self.half, o], self.base + 8, self.par == c)
            for k in range(2):
                self._go(k, 1, z == c + 2 * k)

        def relay(self, k, item):
            src = c + 2 * k
            q = c if item == 0 else o
            arrived(self.out.at[k, q], self.base + 2 * k + item, z > src)
            arrived(self.out.at[k, q], self.base + 4 + 2 * k + item, z < src)
            self._go(k, item, z != src)

    wo_line = Line(s.wo)
    wo_line.start()

    s.wqt[pl.ds(3 * nh * HEAD, 640 - 3 * nh * HEAD), :] = jnp.zeros((640 - 3 * nh * HEAD, D), BF)
    s.brow[...] = jnp.zeros((1, 640), F32)
    s.brow[:, 0:192] = qvb_ref[0:1, :]
    s.brow[:, 384:576] = qvb_ref[1:2, :]
    g1 = g1_ref[...]
    b1 = b1_ref[...]

    def norm1(j):
        def body(i, _):
            rows = pl.ds(pl.multiple_of(i * 32, 32), 32)
            n, _inv = normed(s.x[j, rows, :].astype(F32))
            s.act1[j, rows, :] = (n * g1 + b1).astype(BF)
            return 0

        lax.fori_loop(0, 4, body, 0)

    norm1(c)
    norm1(2 + c)
    for k in range(2):
        arrived(s.x.at[2 * k + o], sx + k)
    norm1(o)
    norm1(2 + o)
    loads["wqt"].wait()
    s.pre[:, 0:640] = dg(s.act1[...].reshape(N, D), s.wqt[...], 1, 1)

    def split(i, _):
        rows = pl.ds(pl.multiple_of(i * 64, 64), 64)
        low = lax.broadcasted_iota(jnp.int32, (64, 128), 1) < HEAD
        t = [s.pre[rows, 128 * j:128 * (j + 1)] + s.brow[:, 128 * j:128 * (j + 1)] for j in range(5)]
        zero = jnp.zeros((64, 128), F32)
        s.q[0, rows, :] = (jnp.where(low, t[0], zero) * 0.125).astype(BF)
        s.q[1, rows, :] = (jnp.where(low, roll64(t[0]), zero) * 0.125).astype(BF)
        s.q[2, rows, :] = (jnp.where(low, t[1], zero) * 0.125).astype(BF)
        s.kv[g, 0, rows, :] = jnp.where(low, roll64(t[1]), roll64(t[3])).astype(BF)
        s.kv[g, 1, rows, :] = jnp.where(low, t[2], t[3]).astype(BF)
        s.kv[g, 2, rows, :] = jnp.where(low, roll64(t[2]), roll64(t[4])).astype(BF)
        return 0

    lax.fori_loop(0, 8, split, 0)

    half_a = pl.ds(0, 256)
    half_b = pl.ds(256, 256)
    skv = new(NG + 1)
    direct = [1, 2] if NG == 4 else list(range(1, NG))
    for t in direct:
        send(s.kv.at[g], s.kv.at[g], skv + t, (2 * peers[t] + c, z))

    loads["cot"].wait()
    for k in range(2):
        s.stage[1, k] = s.cot_raw[other[k]]
        send(s.stage.at[1, k], s.cot.at[2 * k + c], sx + 2 + k, (mate, z))
    for k in range(2):
        s.cot[2 * k + c] = s.cot_raw[own[k]]

    for i in range(2 * nh):
        s.m[i] = jnp.full((1, 256), NEG, F32)
        s.l[i] = jnp.zeros((1, 256), F32)
        s.acc[i] = jnp.zeros((128, 256), F32)

    def masks(src):
        k_low = (low_pos(2 * src), low_pos(2 * src + 1))
        i0 = lax.broadcasted_iota(jnp.int32, (256, 256), 0)
        i1 = lax.broadcasted_iota(jnp.int32, (256, 256), 1)

        def token(i, a, b):
            return i + jnp.where(i < BLK, a * BLK, b * BLK - BLK)

        last = 2 * R - 1
        s.mlo[...] = jnp.where(token(i0, *k_low) <= token(i1, *q_low), 0.0, NEG)
        s.mhi[...] = jnp.where(
            token(i0, last - k_low[0], last - k_low[1])
            <= token(i1, last - q_low[0], last - q_low[1]), 0.0, NEG)

    def attend(src):
        masks(src)

        def body(h, _):
            klo = s.kv[src, h, 0:256, :]
            khi = s.kv[src, h, 256:512, :]
            s1 = dg(klo, s.q[h, 0:256, :], 1, 1) + s.mlo[...]
            old = s.m[2 * h]
            now = jnp.maximum(old, jnp.max(s1, axis=0, keepdims=True))
            e1 = jnp.exp(s1 - now)
            f = jnp.exp(old - now)
            s.l[2 * h] = s.l[2 * h] * f + jnp.sum(e1, axis=0, keepdims=True)
            s.acc[2 * h] = s.acc[2 * h] * f + dg(klo, e1.astype(BF), 0, 0)
            s.m[2 * h] = now
            qhi = s.q[h, 256:512, :]
            s2 = dg(klo, qhi, 1, 1)
            s3 = dg(khi, qhi, 1, 1) + s.mhi[...]
            old = s.m[2 * h + 1]
            now = jnp.maximum(old, jnp.maximum(jnp.max(s2, axis=0, keepdims=True),
                                               jnp.max(s3, axis=0, keepdims=True)))
            e2 = jnp.exp(s2 - now)
            e3 = jnp.exp(s3 - now)
            f = jnp.exp(old - now)
            s.l[2 * h + 1] = (s.l[2 * h + 1] * f + jnp.sum(e2, axis=0, keepdims=True)
                              + jnp.sum(e3, axis=0, keepdims=True))
            s.acc[2 * h + 1] = (s.acc[2 * h + 1] * f + dg(klo, e2.astype(BF), 0, 0)
                                + dg(khi, e3.astype(BF), 0, 0))
            s.m[2 * h + 1] = now
            return 0

        lax.fori_loop(0, nh, body, 0)

    attend(g)
    wo_line.step(1)
    if NG == 4:
        arrived(s.kv.at[peers[1]], skv + 1)
        send(s.kv.at[peers[1], :, half_a], s.kv.at[peers[1], :, half_a], skv + 3, (2 * peers[2] + c, z))
        arrived(s.kv.at[peers[2]], skv + 2)
        send(s.kv.at[peers[2], :, half_b], s.kv.at[peers[2], :, half_b], skv + 4, (2 * peers[1] + c, z))
        attend(peers[1])
        wo_line.step(2)
        attend(peers[2])
        wo_line.step(3)
        arrived(s.kv.at[peers[3], :, half_a], skv + 3)
        arrived(s.kv.at[peers[3], :, half_b], skv + 4)
        attend(peers[3])
    else:
        for t in range(1, NG):
            arrived(s.kv.at[sources[t]], skv + t)

        def rest(t, _):
            attend(lax.rem(g + t, NG))
            return 0

        lax.fori_loop(1, NG, rest, 0)
        wo_line.step(2)
        wo_line.step(3)

    low = lax.broadcasted_iota(jnp.int32, (256, 128), 1) < HEAD
    thirds = []
    for half in range(2):
        rows = pl.ds(256 * half, 256)
        outs = []
        for h in range(nh):
            outs.append(jnp.transpose(s.acc[2 * h + half] / s.l[2 * h + half]))
            s.attp[h, rows, :] = outs[h].astype(BF)
            s.m[2 * h + half] = s.m[2 * h + half] + jnp.log(s.l[2 * h + half])
        pair = jnp.where(low, roll64(outs[0]), outs[1]).astype(BF)
        s.ab[z, rows, :] = pair
        s.attn[rows, 0:128] = pair
        turned = roll64(outs[2])
        s.attn[rows, 128:256] = jnp.where(low, turned, 0.0).astype(BF)
        thirds.append((turned, outs[2]))
    s.ab[z, 512:768, :] = jnp.where(low, thirds[0][0], thirds[1][1]).astype(BF)
    ab_line = Line(s.ab)
    ab_line.start()

    for k in range(2):
        arrived(s.cot.at[2 * k + o], sx + 2 + k)
    loads["pw"].wait()
    for half in range(2):
        s.ga[256 * half:256 * half + 256, :] = dg(
            s.cot[2 * half:2 * half + 2].reshape(256, D), s.pw[...], 1, 1)
    s.wopad[...] = jnp.zeros((nh * BLK, D), BF)
    for h in range(nh):
        s.wopad[BLK * h + HEAD:BLK * h + BLK, :] = s.wo[z, HEAD * h:HEAD * h + HEAD, :]
    zeros = jnp.zeros((HEAD, D), BF)
    for t in range(T):
        s.wolo[t, 0:HEAD, :] = s.wo[t, 128:192, :]
        s.wolo[t, HEAD:BLK, :] = zeros
        s.wohi[t, 0:HEAD, :] = zeros
        s.wohi[t, HEAD:BLK, :] = s.wo[t, 128:192, :]
    for k in range(1, T):
        ab_line.step(k)

    left = jnp.concatenate([s.ab[t, 0:512, :] for t in range(T)], axis=1)
    s.hid[...] = dg(left, s.wo[:, 0:128, :].reshape(T * 128, D), 1, 0)
    tail = jnp.concatenate([s.ab[t, 512:768, :] for t in range(T)], axis=1)
    s.hid[0:256, :] += dg(tail, s.wolo[...].reshape(T * 128, D), 1, 0)
    s.hid[256:512, :] += dg(tail, s.wohi[...].reshape(T * 128, D), 1, 0)
    g2 = g2_ref[...]
    b2 = b2_ref[...]
    ob = ob_ref[...]

    def norm2(i, _):
        rows = pl.ds(pl.multiple_of(i * 32, 32), 32)
        j = lax.div(i, 4)
        sub = pl.ds(pl.multiple_of(lax.rem(i, 4) * 32, 32), 32)
        x = s.x[j, sub, :].astype(F32) + s.hid[rows, :] + ob
        s.hid[rows, :] = x
        n, _inv = normed(x)
        s.act2[rows, :] = (n * g2 + b2).astype(BF)
        return 0

    lax.fori_loop(0, 16, norm2, 0)

    loads["fc"].wait()
    fcb = fcb_ref[...]
    fold1 = Fold(s.p1, s.r1, s.l1)
    fold2 = Fold(s.p2, s.r2, s.l2)
    fold3 = Fold(s.p3, s.r3, s.l3)
    bias_sum = jnp.zeros((8, F), F32)
    for half in range(2):
        base = 256 * half
        s.pre[base:base + 256, :] = dg(s.act2[base:base + 256, :], s.fc[...], 1, 0)

        def gelu(i, total, base=base):
            rows = pl.ds(pl.multiple_of(base + i * 16, 16), 16)
            v = s.pre[rows, :] + fcb
            square = v * v
            th = jnp.tanh(C0 * (v + C1 * square * v))
            one = 1.0 + th
            s.actd[rows, :] = (0.5 * v * one).astype(BF)
            slope = 0.5 * one + (0.5 * v) * (1.0 - th * th) * (C0 * (1.0 + 3.0 * C1 * square))
            grad = slope * s.ga[rows, :]
            s.gpre[rows, :] = grad.astype(BF)
            return total + fold8(grad)

        bias_sum = lax.fori_loop(0, 16, gelu, bias_sum)
        back = dg(s.gpre[base:base + 256, :], s.fc[...], 1, 1)
        s.p1[2 * half] = back[0:128].astype(BF)
        s.p1[2 * half + 1] = back[128:256].astype(BF)
        if half == 0:
            fold1.begin_left(0)
            fold1.begin_left(1)
        else:
            for d in (3, 2):
                fold1.begin_right(d)
            fold1.begin_right(1)
            fold1.begin_left(2)
    s.vsum[...] = jnp.zeros((16, D), F32)
    s.vsum[8:9, :] = jnp.sum(bias_sum, axis=0, keepdims=True)

    sw1 = new(1 + 2 * NG + 1)

    def weight(dst, index, lhs, rhs):
        for i in range(3):
            part = dg(lhs[:, 256 * i:256 * i + 256], rhs, 0, 0).astype(BF)
            lo, hi = 256 * i, 256 * i + 256
            for qd in range(NG):
                a, b = max(lo, qd * Q1), min(hi, qd * Q1 + Q1)
                if a < b:
                    dst[index, qd, a - qd * Q1:b - qd * Q1, :] = part[a - lo:b - lo]

    weight(s.w1, 0, s.actd, s.cot[...].reshape(N, D))
    fold1.step(0)
    weight(s.w1, 1, s.act2, s.gpre[...])
    send(s.w1.at[o], s.w1r, sw1, (mate, z))
    fold1.step(1)
    fold1.step(2)

    fold1.total()
    zrow = pl.multiple_of(z * BLK, BLK)

    def back2(i, sums):
        rows = pl.ds(pl.multiple_of(i * 16, 16), 16)
        n, inv = normed(s.hid[pl.ds(pl.multiple_of(zrow + i * 16, 16), 16), :])
        grad = s.tot[rows, :]
        up = s.cot[z, rows, :].astype(F32)
        qg = grad * g2
        gh = up + inv * (qg - jnp.mean(qg, axis=-1, keepdims=True)
                         - n * jnp.mean(qg * n, axis=-1, keepdims=True))
        s.gh[rows, :] = gh
        s.h[z, rows, :] = gh.astype(BF)
        return (sums[0] + fold8(grad * n), sums[1] + fold8(grad), sums[2] + fold8(gh),
                sums[3] + fold8(up))

    z8 = jnp.zeros((8, D), F32)
    sums = lax.fori_loop(0, 8, back2, (z8, z8, z8, z8))
    h_line = Line(s.h)
    h_line.start()
    for i in range(4):
        s.vsum[2 + i:3 + i, :] = jnp.sum(sums[i], axis=0, keepdims=True)

    for half in range(2):
        base = 256 * half
        fwd = dg(s.actd[base:base + 256, :], s.pw[...], 1, 0)
        s.p2[2 * half] = fwd[0:128].astype(BF)
        s.p2[2 * half + 1] = fwd[128:256].astype(BF)

    def add_into(buf, index, extra):
        def body(i, _):
            buf[index, i] = (buf[index, i].astype(F32) + extra[i].astype(F32)).astype(BF)
            return 0

        lax.fori_loop(0, NG, body, 0)

    arrived(s.w1r, sw1)
    add_into(s.w1, c, s.w1r)
    for t in range(1, NG):
        send(s.w1.at[c, peers[t]], s.w1s.at[t], sw1 + t, (2 * peers[t] + c, z))
    for k in range(1, T):
        h_line.step(k)
    for d in (3, 2, 1):
        fold2.begin_right(d)
        fold2.begin_left(T - 1 - d)

    grads = dg(s.h[...].reshape(N, D), s.wopad[...], 1, 1)
    for h in range(nh):
        s.do[h] = grads[:, 128 * h:128 * h + 128].astype(BF)
    for h in range(nh):
        for half in range(2):
            rows = pl.ds(256 * half, 256)
            both = s.do[h, rows, :].astype(F32) * s.attp[h, rows, :].astype(F32)
            s.delta[2 * h + half] = jnp.sum(jnp.transpose(both), axis=0, keepdims=True)
    for i in range(2 * nh):
        s.acc[i] = jnp.zeros((128, 256), F32)

    def attend_back(src):
        masks(src)

        def body(h, _):
            klo = s.kv[src, h, 0:256, :]
            khi = s.kv[src, h, 256:512, :]

            def tile(k, half, mask):
                qs = s.q[h, 256 * half:256 * half + 256, :]
                ds_ = s.do[h, 256 * half:256 * half + 256, :]
                sc = dg(k, qs, 1, 1)
                if mask is not None:
                    sc = sc + mask[...]
                p = jnp.exp(sc - s.m[2 * h + half])
                d = p * (dg(k, ds_, 1, 1) - s.delta[2 * h + half])
                p = p.astype(BF)
                d = d.astype(BF)
                return d, dg(d, qs, 1, 0) + dg(p, ds_, 1, 0)

            d1, k1 = tile(klo, 0, s.mlo)
            s.acc[2 * h] += dg(klo, d1, 0, 0)
            d2, k2 = tile(klo, 1, None)
            s.dk[src, h, 0:256, :] = (k1 + k2).astype(BF)
            d3, k3 = tile(khi, 1, s.mhi)
            s.dk[src, h, 256:512, :] = k3.astype(BF)
            s.acc[2 * h + 1] += dg(klo, d2, 0, 0) + dg(khi, d3, 0, 0)
            return 0

        lax.fori_loop(0, nh, body, 0)

    sdk = new(NG + 2)

    def w1_gather():
        def body(i, _):
            rows = pl.ds(pl.multiple_of(i * (Q1 // 3), Q1 // 3), Q1 // 3)
            total = s.w1[c, g, rows, :].astype(F32)
            for t in range(1, NG):
                total = total + s.w1s[t, rows, :].astype(F32)
            s.w1f[c, g, rows, :] = total.astype(BF)
            return 0

        for t in range(1, NG):
            arrived(s.w1s.at[t], sw1 + t)
        lax.fori_loop(0, 3, body, 0)
        for t in range(1, NG):
            send(s.w1f.at[c, g], s.w1f.at[c, g], sw1 + NG + t, (2 * peers[t] + c, z))

    spread_o = Spread(s.osh, s.fo)
    pb = pb_ref[...]

    def finish_output():
        fold2.total()

        def body(i, _):
            rows = pl.ds(pl.multiple_of(i * 32, 32), 32)
            y = s.hid[pl.ds(pl.multiple_of(zrow + i * 32, 32), 32), :] + s.tot[rows, :] + pb
            s.osh[rows, :] = y.astype(BF)
            return 0

        lax.fori_loop(0, 4, body, 0)
        spread_o.start()

    if NG == 4:
        attend_back(peers[3])
        send(s.dk.at[peers[3], :, half_a], s.dka.at[0], sdk + 0, (2 * peers[1] + c, z))
        send(s.dk.at[peers[3], :, half_b], s.dka.at[1], sdk + NG, (2 * peers[2] + c, z))
        attend_back(peers[1])
        fold2.step(0)
        w1_gather()
        attend_back(peers[2])
        fold2.step(1)
        arrived(s.dka.at[0], sdk + 0)
        for h in range(nh):
            s.dk[peers[2], h, half_a, :] = (s.dk[peers[2], h, half_a, :].astype(F32)
                                            + s.dka[0, h].astype(F32)).astype(BF)
        send(s.dk.at[peers[2]], s.dkr.at[2], sdk + 2, (2 * peers[2] + c, z))
        arrived(s.dka.at[1], sdk + NG)
        for h in range(nh):
            s.dk[peers[1], h, half_b, :] = (s.dk[peers[1], h, half_b, :].astype(F32)
                                            + s.dka[1, h].astype(F32)).astype(BF)
        send(s.dk.at[peers[1]], s.dkr.at[1], sdk + 1, (2 * peers[1] + c, z))
        attend_back(g)
        fold2.step(2)
        finish_output()
    else:
        def rest_back(t, _):
            attend_back(lax.rem(g + t, NG))
            return 0

        lax.fori_loop(0, NG, rest_back, 0)
        for t in range(1, NG):
            send(s.dk.at[peers[t]], s.dkr.at[t], sdk + t, (2 * peers[t] + c, z))
        w1_gather()
        for j in range(T - 1):
            fold2.step(j)
        finish_output()

    sw2 = new(1 + 2 * NG + 1)

    def put2(first, value, rows):
        for i in range(rows // Q2):
            at = (first + i * Q2) // Q2
            s.w2[at // NG, at % NG] = value[i * Q2:i * Q2 + Q2].astype(BF)

    for half in range(1):
        gout = dg(s.attn[...], s.h[...].reshape(N, D), 0, 0)
        put2(3 * nh * HEAD, gout, nh * HEAD)
    spread_o.swapped()

    got = [1, 2] if NG == 4 else list(range(1, NG))
    for t in got:
        arrived(s.dkr.at[t], sdk + t)
    col = [jnp.zeros((1, 128), F32) for _ in range(5)]
    for half in range(2):
        rows = pl.ds(256 * half, 256)
        dq = [jnp.transpose(s.acc[2 * h + half]) * 0.125 for h in range(nh)]
        dkv = []
        for h in range(nh):
            total = s.dk[g, h, rows, :].astype(F32)
            for t in got:
                total = total + s.dkr[t, h, rows, :].astype(F32)
            dkv.append(total)
        tiles = [
            jnp.where(low, dq[0], roll64(dq[1])),
            jnp.where(low, dq[2], roll64(dkv[0])),
            jnp.where(low, dkv[1], roll64(dkv[2])),
            jnp.where(low, roll64(dkv[0]), dkv[1]),
            jnp.where(low, roll64(dkv[2]), 0.0),
        ]
        for j in range(5):
            col[j] = col[j] + jnp.sum(tiles[j], axis=0, keepdims=True)
            s.gn[rows, 128 * j:128 * j + 128] = tiles[j].astype(BF)
            s.gt[128 * j:128 * j + 128, 256 * half:256 * half + 256] = jnp.transpose(tiles[j]).astype(BF)
    for j in range(5):
        s.vsum[9:10, 128 * j:128 * j + 128] = col[j]

    for half in range(2):
        base = 256 * half
        back = dg(s.gn[base:base + 256, :], s.wqt[...], 1, 0)
        s.p3[2 * half] = back[0:128].astype(BF)
        s.p3[2 * half + 1] = back[128:256].astype(BF)
        if half == 0:
            fold3.begin_left(0)
            fold3.begin_left(1)
        else:
            for d in (3, 2):
                fold3.begin_right(d)
            fold3.begin_right(1)
            fold3.begin_left(2)

    for i in range(3):
        put2(192 * i, dg(s.gt[192 * i:192 * i + 192, :], s.act1[...].reshape(N, D), 1, 0), 192)
    send(s.w2.at[o], s.w2r, sw2, (mate, z))
    fold3.step(0)
    arrived(s.w2r, sw2)
    add_into(s.w2, c, s.w2r)
    for t in range(1, NG):
        send(s.w2.at[c, peers[t]], s.w2s.at[t], sw2 + t, (2 * peers[t] + c, z))
    fold3.step(1)
    fold3.step(2)

    fold3.total()

    def back1(i, sums):
        rows = pl.ds(pl.multiple_of(i * 16, 16), 16)
        n, inv = normed(s.x[z, rows, :].astype(F32))
        grad = s.tot[rows, :]
        qg = grad * g1
        gx = s.gh[rows, :] + inv * (qg - jnp.mean(qg, axis=-1, keepdims=True)
                                    - n * jnp.mean(qg * n, axis=-1, keepdims=True))
        s.gsh[rows, :] = gx.astype(BF)
        return (sums[0] + fold8(grad * n), sums[1] + fold8(grad))

    sums = lax.fori_loop(0, 8, back1, (z8, z8))
    spread_g = Spread(s.gsh, s.fg)
    spread_g.start()
    for i in range(2):
        s.vsum[i:i + 1, :] = jnp.sum(sums[i], axis=0, keepdims=True)

    svz = new(T)
    s.vz[z] = s.vsum[...].astype(BF)
    for t in range(1, T):
        send(s.vz.at[z], s.vz.at[z], svz + t, (r, lax.rem(z + t, T)))

    for k in range(2):
        spread_o.relay(k, 0)
    for k in range(2):
        spread_o.relay(k, 1)
    spread_g.swapped()

    def w2_gather():
        for t in range(1, NG):
            arrived(s.w2s.at[t], sw2 + t)
        total = s.w2[c, g].astype(F32)
        for t in range(1, NG):
            total = total + s.w2s[t].astype(F32)
        s.w2f[c, g] = total.astype(BF)
        for t in range(1, NG):
            send(s.w2f.at[c, g], s.w2f.at[c, g], sw2 + NG + t, (2 * peers[t] + c, z))

    w2_gather()
    for t in range(1, NG):
        arrived(s.w1f.at[c, sources[t]], sw1 + NG + t)
    send(s.w1f.at[c], s.w1f.at[c], sw1 + 2 * NG, (mate, z))

    for t in range(1, T):
        arrived(s.vz.at[lax.rem(z + T - t, T)], svz + t)
    svc = new(R)
    upper = s.vz[0, 0:8, :].astype(F32)
    for t in range(1, T):
        upper = upper + s.vz[t, 0:8, :].astype(F32)
    s.vc[r] = jnp.concatenate([upper, s.vsum[8:16, :]], axis=0).astype(BF)
    for t in range(1, R):
        send(s.vc.at[r], s.vc.at[r], svc + t, (lax.rem(r + t, R), z))

    for k in range(2):
        spread_g.relay(k, 0)
    for k in range(2):
        spread_g.relay(k, 1)
    for t in range(1, NG):
        arrived(s.w2f.at[c, sources[t]], sw2 + NG + t)
    send(s.w2f.at[c], s.w2f.at[c], sw2 + 2 * NG, (mate, z))
    for t in range(1, R):
        arrived(s.vc.at[lax.rem(r + R - t, R)], svc + t)
    total = s.vc[0].astype(F32)
    for t in range(1, R):
        total = total + s.vc[t].astype(F32)
    s.vsum[...] = total
    arrived(s.w1f.at[o], sw1 + 2 * NG)
    outs = [pltpu.make_async_copy(s.fo, fo_out, s.ls.at[6]), pltpu.make_async_copy(s.fg, fg_out, s.ls.at[7]),
            pltpu.make_async_copy(s.w1f, w1_out, s.ls.at[8]), pltpu.make_async_copy(s.vsum, v_out, s.ls.at[10])]
    for copy in outs:
        copy.start()
    arrived(s.w2f.at[o], sw2 + 2 * NG)
    last = pltpu.make_async_copy(s.w2f, w2_out, s.ls.at[9])
    last.start()
    for cond, done in pending:
        if cond is None:
            done()
        else:
            pl.when(cond)(done)
    for copy in outs:
        copy.wait()
    last.wait()


def finish_kernel(R, NS, pos_ref, seq_ref, rank_ref, w1_ref, w2_ref, fo_ref, fg_ref, v_ref, out_ref, gt_ref,
                  ln1g_ref, ln1b_ref, gq_ref, gqv_ref, go_ref, ob_ref, ln2g_ref, ln2b_ref, gf_ref, fb_ref,
                  gp_ref, pb_ref):
    i = pl.program_id(0)
    gp_ref[...] = w1_ref[0].astype(F32)
    gf_ref[...] = w1_ref[1].astype(F32)

    @pl.when(i < 6)
    def _():
        gq_ref[...] = w2_ref[...].astype(F32)

    @pl.when(i >= 6)
    def _():
        go_ref[...] = w2_ref[...].astype(F32)

    @pl.when(i < 4)
    def _():
        b = 4 * rank_ref[0] + i
        high = jnp.where(pos_ref[b] < R, 0, 1)
        out_ref[...] = fo_ref[high, seq_ref[b]]
        gt_ref[...] = fg_ref[high, seq_ref[b]]

    @pl.when(i == 0)
    def _():
        ln1g_ref[...] = v_ref[0:1, :]
        ln1b_ref[...] = v_ref[1:2, :]
        ln2g_ref[...] = v_ref[2:3, :]
        ln2b_ref[...] = v_ref[3:4, :]
        ob_ref[...] = v_ref[4:5, :]
        pb_ref[...] = v_ref[5:6, :]
        fb_ref[...] = v_ref[8:9, :]
        gqv_ref[0:1, :] = v_ref[9:10, 0:192]
        gqv_ref[1:2, :] = v_ref[9:10, 384:576]


def per_device(R, T, tokens, cotangent, block_pos, block_seq, ln1_gain, ln1_bias, qkv_weight, qv_bias,
               out_weight, out_bias, ln2_gain, ln2_bias, fc_weight, fc_bias, proj_weight, proj_bias):
    D = tokens.shape[1]
    F = fc_weight.shape[1]
    local = qkv_weight.shape[2]
    nh = local // HEAD
    NG = R // 2
    sizes = scratch_list(R, T, D, F, nh)
    names = [n for n, _ in sizes]
    row = lambda v: v.reshape(1, -1)
    wqt = jnp.transpose(qkv_weight, (1, 2, 0)).reshape(3 * local, D)
    sm = pl.BlockSpec(memory_space=pltpu.SMEM)
    vm = pl.BlockSpec(memory_space=pltpu.VMEM)
    hb = pl.BlockSpec(memory_space=pl.ANY)
    w1, w2, fo, fg, vs = pl.pallas_call(
        functools.partial(layer_kernel, R, T, D, F, nh, names),
        out_shape=(
            jax.ShapeDtypeStruct((2, NG, D // NG, D), BF),
            jax.ShapeDtypeStruct((2, NG, D // 2 // NG, D), BF),
            jax.ShapeDtypeStruct((2, 2, BLK, D), BF),
            jax.ShapeDtypeStruct((2, 2, BLK, D), BF),
            jax.ShapeDtypeStruct((16, D), F32),
        ),
        in_specs=[sm, sm, hb, hb, vm, vm, hb, vm, hb, vm, vm, vm, hb, vm, hb, vm],
        out_specs=(hb, hb, hb, hb, hb),
        scratch_shapes=[sp for _, sp in sizes],
        compiler_params=pltpu.CompilerParams(
            collective_id=0, has_side_effects=True, vmem_limit_bytes=67043328),
        name="layer",
    )(block_pos, block_seq, tokens.reshape(4, BLK, D), cotangent.reshape(4, BLK, D), row(ln1_gain),
      row(ln1_bias), wqt, qv_bias, out_weight, row(out_bias), row(ln2_gain), row(ln2_bias), fc_weight,
      row(fc_bias), proj_weight, row(proj_bias))

    rank = lax.axis_index("ctx").astype(jnp.int32).reshape(1)
    NS = 8
    rb = D // NS
    whole = lambda *shape: pl.BlockSpec(shape, lambda i: (0,) * len(shape))
    vec = jax.ShapeDtypeStruct((1, D), F32)
    outs = pl.pallas_call(
        functools.partial(finish_kernel, R, NS),
        grid=(NS,),
        out_shape=(
            jax.ShapeDtypeStruct((4 * BLK, D), BF),
            jax.ShapeDtypeStruct((4 * BLK, D), BF),
            vec, vec,
            jax.ShapeDtypeStruct((3 * local, D), F32),
            jax.ShapeDtypeStruct((2, local), F32),
            jax.ShapeDtypeStruct((local, D), F32),
            vec, vec, vec,
            jax.ShapeDtypeStruct((D, F), F32),
            vec,
            jax.ShapeDtypeStruct((F, D), F32),
            vec,
        ),
        in_specs=[sm, sm, sm,
                  pl.BlockSpec((2, rb, D), lambda i: (0, i, 0)),
                  pl.BlockSpec((rb, D), lambda i: (i, 0)),
                  whole(2, 2, BLK, D), whole(2, 2, BLK, D), whole(16, D)],
        out_specs=(
            pl.BlockSpec((BLK, D), lambda i: (jnp.minimum(i, 3), 0)),
            pl.BlockSpec((BLK, D), lambda i: (jnp.minimum(i, 3), 0)),
            whole(1, D), whole(1, D),
            pl.BlockSpec((rb, D), lambda i: (jnp.minimum(i, 5), 0)),
            whole(2, local),
            pl.BlockSpec((rb, D), lambda i: (jnp.maximum(i - 6, 0), 0)),
            whole(1, D), whole(1, D), whole(1, D),
            pl.BlockSpec((rb, F), lambda i: (i, 0)),
            whole(1, F),
            pl.BlockSpec((rb, D), lambda i: (i, 0)),
            whole(1, D),
        ),
        name="finish",
    )(block_pos, block_seq, rank, w1.reshape(2, D, D), w2.reshape(D, D), fo, fg, vs)
    (output, grad_tokens, ln1g, ln1b, gq, gqv, go, ob, ln2g, ln2b, gf, fb, gp, pb) = outs
    flat = lambda v: v.reshape(-1)
    return (output, grad_tokens, flat(ln1g), flat(ln1b),
            jnp.transpose(gq.reshape(3, local, D), (2, 0, 1)), gqv, go, flat(ob), flat(ln2g), flat(ln2b),
            gf, flat(fb), gp, flat(pb))


def solution(mesh):
    R = mesh.shape["ctx"]
    T = mesh.shape["tp"]
    return jax.shard_map(
        functools.partial(per_device, R, T),
        mesh=mesh,
        in_specs=(
            P("ctx", None), P("ctx", None), P(), P(), P(), P(), P(None, None, "tp"), P(None, "tp"),
            P("tp", None), P(), P(), P(), P(None, "tp"), P("tp"), P("tp", None), P(),
        ),
        out_specs=(
            P("ctx", None), P("ctx", None), P(), P(), P(None, None, "tp"), P(None, "tp"), P("tp", None),
            P(), P(), P(), P(None, "tp"), P("tp"), P("tp", None), P(),
        ),
        check_vma=False,
    )
```

profile of v0, /device:TPU:1, one launch (start us, length us, event | category | flops | bytes accessed | tf_op | source)
XLA Modules:
  0.0 218.5 jit_solution(1677241977142903925)
XLA Ops:
  0.6 1.3 reshape.94.refs_4_
  1.9 1.3 reshape.95.refs_5_
  3.2 1.3 reshape.97.refs_9_
  4.5 1.3 reshape.98.refs_10_
  5.7 1.3 reshape.99.refs_11_
  7.0 1.3 reshape.100.refs_13_
  8.3 1.3 reshape.101.refs_15_
  9.5 191.9 %layer.1 = (bf16[2,4,192,768]{3,2,1,0:T(8,128)(2,1)}, bf16[2,4,96,768]{3,2,1,0:T(8,128)(2,1)}, bf16[2,2,128,768]{3,2,1,0:T(8,128)(2,1)}, bf16[2,2,128,768]{3,2,1,0:T(8,128)(2,1)}, f32[16,768]{1,0:T(8,128)}) custom-call(s32[32]{0:T(128)} %pos_ref.1, s32[32]{0:T(128)} %seq_ref.1, bf16[4,128,768]{2,1,0:T(8,128)(2,1)} %bitcast.14, ...), custom_call_target="tpu_custom_call" | custom-call | tf_op jit(solution)/shard_map/layer/pallas_call | solution.py:928
  201.5 8.1 %finish.1 = (bf16[512,768]{1,0:T(8,128)(2,1)}, bf16[512,768]{1,0:T(8,128)(2,1)}, f32[1,768]{1,0:T(1,128)}, f32[1,768]{1,0:T(1,128)}, f32[576,768]{1,0:T(8,128)},...) custom-call(s32[32]{0:T(128)} %pos_ref.1, ...), custom_call_target="tpu_custom_call" | custom-call | tf_op jit(solution)/shard_map/finish/pallas_call | solution.py:952
  209.6 1.3 reduce
  210.9 1.3 reduce.1
  212.1 1.3 reduce.2
  213.4 1.3 reduce.3
  214.7 1.3 reduce.4
  216.0 1.3 reduce.5
  217.3 1.3 reduce.6
where the time goes:
time: 221 us; the launch traced here: 219 us
  Pallas kernels  200 us (90%)
  other arithmetic  8.96 us (4%)
  local copies, waits for them, and re-layouts  8.87 us (4%)
    pallas_call x1, Pallas kernels, per_device(): pl.pallas_call(functools.partial(layer_kernel, R, T, D, F, nh, names), ou...  192 us
    pallas_call x7, other arithmetic, per_device(): pl.pallas_call(functools.partial(finish_kernel, R, NS), grid=(NS,), out_s...  8.96 us
    reshape x7, local copies, waits for them, and re-layouts, per_device(): row = lambda v: v.reshape(1, -1)  8.87 us
    pallas_call x1, Pallas kernels, per_device(): pl.pallas_call(functools.partial(finish_kernel, R, NS), grid=(NS,), out_s...  8.11 us

commit v1 on v0

v1 whole, which is shorter than its diff:
```python
import functools
from types import SimpleNamespace

import jax
import jax.numpy as jnp
from jax import lax
from jax.experimental import pallas as pl
from jax.experimental.pallas import tpu as pltpu
from jax.sharding import PartitionSpec as P

HEAD = 64
BLK = 128
BF = jnp.bfloat16
F32 = jnp.float32
MESH = pl.DeviceIdType.MESH
NEG = -1e30
C0 = 0.7978845608028654
C1 = 0.044715
U = 2
SEMS = 160


def dg(a, b, ca, cb):
    return lax.dot_general(a, b, (((ca,), (cb,)), ((), ())), preferred_element_type=F32)


def normed(x):
    centre = jnp.mean(x, axis=-1, keepdims=True)
    shifted = x - centre
    spread = jnp.mean(shifted * shifted, axis=-1, keepdims=True)
    inverse = lax.rsqrt(spread + 1e-05)
    return shifted * inverse, inverse


def fold8(x):
    rows, width = x.shape
    return jnp.sum(x.reshape(rows // 8, 8, width), axis=0)


def roll64(x):
    return pltpu.roll(x, 64, 1)


def scratch_list(R, T, D, F, nh):
    NG = R // 2
    N = 4 * BLK
    v = pltpu.VMEM
    out = [
        ("tok_raw", v((4, BLK, D), BF)),
        ("cot_raw", v((4, BLK, D), BF)),
        ("stage", v((2, 2, BLK, D), BF)),
        ("x", v((4, BLK, D), BF)),
        ("cot", v((4, BLK, D), BF)),
        ("wqt", v((640, D), BF)),
        ("wo", v((T, 2, nh * HEAD // 2, D), BF)),
        ("wolo", v((T, BLK, D), BF)),
        ("wohi", v((T, BLK, D), BF)),
        ("wopad", v((nh * BLK, D), BF)),
        ("fc", v((D, F), BF)),
        ("pw", v((F, D), BF)),
        ("brow", v((1, 640), F32)),
        ("act1", v((4, BLK, D), BF)),
        ("q", v((nh, N, 128), BF)),
        ("kv", v((NG, 4, nh, BLK, 128), BF)),
        ("pre", v((N, D), F32)),
        ("ga", v((N, F), F32)),
        ("hid", v((4, BLK, D), F32)),
        ("act2", v((N, D), BF)),
        ("actd", v((N, F), BF)),
        ("gpre", v((N, F), BF)),
        ("mlo", v((256, 256), F32)),
        ("mhi", v((256, 256), F32)),
        ("m", v((2 * nh, 1, 256), F32)),
        ("l", v((2 * nh, 1, 256), F32)),
        ("delta", v((2 * nh, 1, 256), F32)),
        ("acc", v((2 * nh, 128, 256), F32)),
        ("attp", v((nh, N, 128), BF)),
        ("attn", v((N, 256), BF)),
        ("ab", v((T, 768, 128), BF)),
        ("p1", v((4, BLK, D), BF)),
        ("r1", v((4, BLK, D), BF)),
        ("l1", v((4, BLK, D), BF)),
        ("p2", v((4, BLK, D), BF)),
        ("r2", v((4, BLK, D), BF)),
        ("l2", v((4, BLK, D), BF)),
        ("p3", v((4, BLK, D), BF)),
        ("r3", v((4, BLK, D), BF)),
        ("l3", v((4, BLK, D), BF)),
        ("gh", v((BLK, D), F32)),
        ("h", v((4, BLK, D), BF)),
        ("do", v((nh, N, 128), BF)),
        ("dk", v((NG, nh, N, 128), BF)),
        ("dkr", v((NG, nh, N, 128), BF)),
        ("dka", v((2, nh, 256, 128), BF)),
        ("gn", v((N, 640), BF)),
        ("w1", v((2, NG, D // NG, D), BF)),
        ("w1r", v((NG, D // NG, D), BF)),
        ("w1s", v((NG, D // NG, D), BF)),
        ("w1f", v((2, NG, D // NG, D), BF)),
        ("w2", v((2, NG, D // 2 // NG, D), BF)),
        ("w2r", v((NG, D // 2 // NG, D), BF)),
        ("w2s", v((NG, D // 2 // NG, D), BF)),
        ("w2f", v((2, NG, D // 2 // NG, D), BF)),
        ("yo", v((4, BLK, D), BF)),
        ("yg", v((4, BLK, D), BF)),
        ("mo", v((2, BLK, D), BF)),
        ("mg", v((2, BLK, D), BF)),
        ("vsum", v((16, D), F32)),
        ("vz", v((T, 16, D), BF)),
        ("vc", v((R, 16, D), BF)),
        ("ss", pltpu.SemaphoreType.DMA((SEMS + 16 * NG,))),
        ("rs", pltpu.SemaphoreType.DMA((SEMS + 16 * NG,))),
        ("ls", pltpu.SemaphoreType.DMA((24,))),
    ]
    return out


def layer_kernel(R, T, D, F, nh, names, *refs):
    (pos_ref, seq_ref, tok_hbm, cot_hbm, g1_ref, b1_ref, wqt_hbm, qvb_ref, wo_hbm, ob_ref, g2_ref,
     b2_ref, fc_hbm, fcb_ref, pw_hbm, pb_ref, w1_out, w2_out, fo_out, fg_out, v_out) = refs[:21]
    s = SimpleNamespace(**dict(zip(names, refs[21:])))
    NG = R // 2
    N = 4 * BLK
    Q1 = D // NG
    Q2 = D // 2 // NG
    RU = BLK // U
    r = lax.axis_index("ctx")
    z = lax.axis_index("tp")
    c = lax.rem(r, 2)
    o = 1 - c
    g = lax.div(r, 2)
    mate = 2 * g + o
    if NG == 4:
        ga_ = g + 1 - 2 * lax.rem(g, 2)
        gb_ = g + 2 - 4 * lax.div(g, 2)
        gc_ = ga_ + 2 - 4 * lax.div(ga_, 2)
        peers = [g, ga_, gb_, gc_]
        sources = peers
    else:
        peers = [lax.rem(g + t, NG) for t in range(NG)]
        sources = [lax.rem(g + NG - t, NG) for t in range(NG)]

    pending = []
    ids = [0]

    def new(count=1):
        first = ids[0]
        ids[0] += count
        assert ids[0] <= SEMS + 16 * NG
        return first

    def remote(src, dst, slot, dev):
        return pltpu.make_async_remote_copy(
            src_ref=src, dst_ref=dst, send_sem=s.ss.at[slot], recv_sem=s.rs.at[slot],
            device_id=dev, device_id_type=MESH)

    def send(src, dst, slot, dev, cond=None):
        def go():
            remote(src, dst, slot, dev).start()

        def done():
            remote(src, dst, slot, dev).wait_send()

        if cond is None:
            go()
        else:
            pl.when(cond)(go)
        pending.append((cond, done))

    def arrived(dst, slot, cond=None):
        def go():
            remote(dst, dst, slot, (r, z)).wait_recv()

        if cond is None:
            go()
        else:
            pl.when(cond)(go)

    loads = {}

    def load(name, src, dst, k):
        loads[name] = pltpu.make_async_copy(src, dst, s.ls.at[k])
        loads[name].start()

    load("tok", tok_hbm, s.tok_raw, 0)
    load("wqt", wqt_hbm, s.wqt.at[pl.ds(0, 3 * nh * HEAD)], 1)
    load("wo", wo_hbm, s.wo.at[z], 3)
    load("cot", cot_hbm, s.cot_raw, 2)
    load("pw", pw_hbm, s.pw, 4)
    load("fc", fc_hbm, s.fc, 5)

    barrier = pltpu.get_barrier_semaphore()
    for t in range(1, R):
        pl.semaphore_signal(barrier, inc=1, device_id=(lax.rem(r + t, R), z), device_id_type=MESH)

    @pl.when(z > 0)
    def _():
        pl.semaphore_signal(barrier, inc=1, device_id=(r, z - 1), device_id_type=MESH)

    @pl.when(z < T - 1)
    def _():
        pl.semaphore_signal(barrier, inc=1, device_id=(r, z + 1), device_id_type=MESH)

    sides = lax.div(z + T - 1, T) + lax.div(2 * T - 2 - z, T)
    pl.semaphore_wait(barrier, R - 1 + sides)

    def find(seq):
        low = jnp.int32(0)
        high = jnp.int32(0)
        for b in range(4):
            same = seq_ref[4 * r + b] == seq
            first = pos_ref[4 * r + b] < R
            low = jnp.where(same & first, b, low)
            high = jnp.where(same & jnp.logical_not(first), b, high)
        return low, high

    def low_pos(rank):
        total = jnp.int32(0)
        for b in range(4):
            here = (seq_ref[4 * rank + b] == c) & (pos_ref[4 * rank + b] < R)
            total = total + jnp.where(here, pos_ref[4 * rank + b], 0)
        return total

    other = find(o)
    own = find(c)
    q_low = (low_pos(2 * g), low_pos(2 * g + 1))

    sx = new(4)
    loads["tok"].wait()
    for k in range(2):
        s.stage[0, k] = s.tok_raw[other[k]]
        send(s.stage.at[0, k], s.x.at[2 * k + c], sx + k, (mate, z))
    for k in range(2):
        s.x[2 * k + c] = s.tok_raw[own[k]]

    class Line:
        def __init__(self, at, pieces, seen=None):
            self.at, self.pieces, self.seen = at, pieces, seen
            self.base = [new(2 * (T - 1)) for _ in range(pieces)]

        def start(self, u):
            a, base = self.at(z, u), self.base[u]
            send(a, a, base, (r, z + 1), z < T - 1)
            send(a, a, base + T - 1, (r, z - 1), z > 0)
            if self.seen is not None:
                self.seen(z, u, None)

        def step(self, u, k):
            base = self.base[u]
            a = jnp.maximum(z - k, 0)
            b = jnp.minimum(z + k, T - 1)
            left, right = self.at(a, u), self.at(b, u)
            arrived(left, base + k - 1, z >= k)
            if k < T - 1:
                send(left, left, base + k, (r, z + 1), (z >= k) & (z < T - 1))
            if self.seen is not None:
                self.seen(a, u, z >= k)
            arrived(right, base + T - 1 + k - 1, z <= T - 1 - k)
            if k < T - 1:
                send(right, right, base + T - 1 + k, (r, z - 1), (z <= T - 1 - k) & (z > 0))
            if self.seen is not None:
                self.seen(b, u, z <= T - 1 - k)

    class Sum:
        def __init__(self, part, from_left, from_right):
            self.part, self.fl, self.fr = part, from_left, from_right
            self.base = [new(2 * T) for _ in range(U)]

            @pl.when(z == 0)
            def _():
                from_left[0] = jnp.zeros((BLK, D), BF)

            @pl.when(z == T - 1)
            def _():
                from_right[T - 1] = jnp.zeros((BLK, D), BF)

        def at(self, buf, d, u):
            return buf.at[d, pl.ds(RU * u, RU)]

        def begin(self, u, ds):
            for d in ds:
                if d > 0:
                    send(self.at(self.part, d, u), self.at(self.fl, d, u), self.base[u] + d, (r, z + 1), z == 0)
                e = T - 1 - d
                if e < T - 1:
                    send(self.at(self.part, e, u), self.at(self.fr, e, u), self.base[u] + T + e, (r, z - 1),
                         z == T - 1)

        def relay(self, u, d, right, where):
            buf, slot = (self.fl, self.base[u] + d) if right else (self.fr, self.base[u] + T + d)
            to = z + 1 if right else z - 1
            cond = z == where

            @pl.when(cond)
            def _():
                arrived(self.at(buf, d, u), slot)
                rows = pl.ds(RU * u, RU)
                self.part[d, rows, :] = (self.part[d, rows, :].astype(F32)
                                         + buf[d, rows, :].astype(F32)).astype(BF)

            send(self.at(self.part, d, u), self.at(buf, d, u), slot, (r, to), cond)

        def hop1(self, u):
            self.relay(u, 3, True, 1)
            self.relay(u, 0, False, 2)
            self.relay(u, 2, True, 1)
            self.relay(u, 1, False, 2)

        def hop2(self, u):
            self.relay(u, 3, True, 2)
            self.relay(u, 0, False, 1)

        def last(self, u):
            arrived(self.at(self.fl, z, u), self.base[u] + z, z > 0)
            arrived(self.at(self.fr, z, u), self.base[u] + T + z, z < T - 1)

        def total(self, rows):
            return (self.part[z, rows, :].astype(F32) + self.fl[z, rows, :].astype(F32)
                    + self.fr[z, rows, :].astype(F32))

    def pieces_of(buf):
        return lambda i, u: buf.at[i, pl.ds(RU * u, RU)]

    class Hand:
        def __init__(self, buf, landing):
            self.buf, self.landing = buf, landing
            self.base = [new(2) for _ in range(U)]

        def __call__(self, i, u, cond):
            k = lax.div(i, 2)
            wanted = lax.rem(i, 2) != c
            if cond is not None:
                wanted = wanted & cond
            send(self.buf.at[i, pl.ds(RU * u, RU)], self.landing.at[k, pl.ds(RU * u, RU)],
                 self.base[u] + k, (mate, z), wanted)

        def wait(self):
            for u in range(U):
                for k in range(2):
                    arrived(self.landing.at[k, pl.ds(RU * u, RU)], self.base[u] + k)

    WH = nh * HEAD // 2
    swo = new(T)

    def hand_wo(i, u, cond):
        send(s.wo.at[i, c], s.wo.at[i, c], swo + i, (mate, z), cond)

    wo_line = Line(lambda i, u: s.wo.at[i, c], 1, lambda i, u, cond: None if cond is None else hand_wo(i, u, cond))
    loads["wo"].wait()
    wo_line.start(0)
    s.wqt[pl.ds(3 * nh * HEAD, 640 - 3 * nh * HEAD), :] = jnp.zeros((640 - 3 * nh * HEAD, D), BF)
    s.brow[...] = jnp.zeros((1, 640), F32)
    s.brow[:, 0:192] = qvb_ref[0:1, :]
    s.brow[:, 384:576] = qvb_ref[1:2, :]
    g1 = g1_ref[...].reshape(1, -1)
    b1 = b1_ref[...].reshape(1, -1)
    skv = new(max(4 * 4, NG + 1))

    def project(first):
        for k in range(2):
            for i in range(2):
                rows = pl.ds(64 * i, 64)
                n, _inv = normed(s.x[2 * k + first, rows, :].astype(F32))
                s.act1[2 * k + first, rows, :] = (n * g1 + b1).astype(BF)
        a = jnp.concatenate([s.act1[first], s.act1[2 + first]], axis=0)
        s.pre[0:256, 0:640] = dg(a, s.wqt[...], 1, 1)
        low = lax.broadcasted_iota(jnp.int32, (BLK, 128), 1) < HEAD
        zero = jnp.zeros((BLK, 128), F32)
        for k in range(2):
            j = 2 * k + first
            t = [s.pre[BLK * k:BLK * k + BLK, 128 * i:128 * i + 128] + s.brow[:, 128 * i:128 * i + 128]
                 for i in range(5)]
            rows = pl.ds(pl.multiple_of(j * BLK, BLK), BLK)
            s.kv[g, j, 0] = jnp.where(low, roll64(t[1]), roll64(t[3])).astype(BF)
            s.kv[g, j, 1] = jnp.where(low, t[2], t[3]).astype(BF)
            s.kv[g, j, 2] = jnp.where(low, roll64(t[2]), roll64(t[4])).astype(BF)
            s.q[0, rows, :] = (jnp.where(low, t[0], zero) * 0.125).astype(BF)
            s.q[1, rows, :] = (jnp.where(low, roll64(t[0]), zero) * 0.125).astype(BF)
            s.q[2, rows, :] = (jnp.where(low, t[1], zero) * 0.125).astype(BF)

    def kv_send(block, t, to):
        send(s.kv.at[block[0], block[1]], s.kv.at[block[0], block[1]], skv + 4 * t + block[1],
             (2 * to + c, z))

    def kv_arrived(src, j, t):
        arrived(s.kv.at[src, j], skv + 4 * t + j)

    loads["wqt"].wait()
    project(c)
    if NG == 4:
        kv_send((g, c), 1, peers[1])
        kv_send((g, 2 + c), 2, peers[2])
        kv_send((g, 2 + c), 1, peers[1])
        kv_send((g, c), 2, peers[2])
    for k in range(2):
        arrived(s.x.at[2 * k + o], sx + k)
    project(o)
    if NG == 4:
        kv_send((g, o), 1, peers[1])
        kv_send((g, 2 + o), 2, peers[2])
        kv_send((g, 2 + o), 1, peers[1])
        kv_send((g, o), 2, peers[2])
    else:
        for t in range(1, NG):
            send(s.kv.at[g], s.kv.at[g], skv + t, (2 * peers[t] + c, z))

    loads["cot"].wait()
    for k in range(2):
        s.stage[1, k] = s.cot_raw[other[k]]
        send(s.stage.at[1, k], s.cot.at[2 * k + c], sx + 2 + k, (mate, z))
    for k in range(2):
        s.cot[2 * k + c] = s.cot_raw[own[k]]
    for i in range(2 * nh):
        s.m[i] = jnp.full((1, 256), NEG, F32)
        s.l[i] = jnp.zeros((1, 256), F32)
        s.acc[i] = jnp.zeros((128, 256), F32)

    def masks(src):
        k_low = (low_pos(2 * src), low_pos(2 * src + 1))
        i0 = lax.broadcasted_iota(jnp.int32, (256, 256), 0)
        i1 = lax.broadcasted_iota(jnp.int32, (256, 256), 1)

        def token(i, a, b):
            return i + jnp.where(i < BLK, a * BLK, b * BLK - BLK)

        last = 2 * R - 1
        s.mlo[...] = jnp.where(token(i0, *k_low) <= token(i1, *q_low), 0.0, NEG)
        s.mhi[...] = jnp.where(
            token(i0, last - k_low[0], last - k_low[1])
            <= token(i1, last - q_low[0], last - q_low[1]), 0.0, NEG)

    def keys_of(src, h):
        return s.kv[src, 0:2, h].reshape(256, 128), s.kv[src, 2:4, h].reshape(256, 128)

    def attend(src):
        masks(src)
        for h in range(nh):
            klo, khi = keys_of(src, h)
            s1 = dg(klo, s.q[h, 0:256, :], 1, 1) + s.mlo[...]
            old = s.m[2 * h]
            now = jnp.maximum(old, jnp.max(s1, axis=0, keepdims=True))
            e1 = jnp.exp(s1 - now)
            f = jnp.exp(old - now)
            s.l[2 * h] = s.l[2 * h] * f + jnp.sum(e1, axis=0, keepdims=True)
            s.acc[2 * h] = s.acc[2 * h] * f + dg(klo, e1.astype(BF), 0, 0)
            s.m[2 * h] = now
            qhi = s.q[h, 256:512, :]
            s2 = dg(klo, qhi, 1, 1)
            s3 = dg(khi, qhi, 1, 1) + s.mhi[...]
            old = s.m[2 * h + 1]
            now = jnp.maximum(old, jnp.maximum(jnp.max(s2, axis=0, keepdims=True),
                                               jnp.max(s3, axis=0, keepdims=True)))
            e2 = jnp.exp(s2 - now)
            e3 = jnp.exp(s3 - now)
            f = jnp.exp(old - now)
            s.l[2 * h + 1] = (s.l[2 * h + 1] * f + jnp.sum(e2, axis=0, keepdims=True)
                              + jnp.sum(e3, axis=0, keepdims=True))
            s.acc[2 * h + 1] = (s.acc[2 * h + 1] * f + dg(klo, e2.astype(BF), 0, 0)
                                + dg(khi, e3.astype(BF), 0, 0))
            s.m[2 * h + 1] = now

    attend(g)
    wo_line.step(0, 1)
    for k in range(2):
        arrived(s.cot.at[2 * k + o], sx + 2 + k)
    loads["pw"].wait()
    for half in range(2):
        s.ga[256 * half:256 * half + 256, :] = dg(
            s.cot[2 * half:2 * half + 2].reshape(256, D), s.pw[...], 1, 1)
    s.wopad[...] = jnp.zeros((nh * BLK, D), BF)
    mine = s.wo[z].reshape(nh * HEAD, D)
    for h in range(nh):
        s.wopad[BLK * h + HEAD:BLK * h + BLK, :] = mine[HEAD * h:HEAD * h + HEAD]
    sum1 = Sum(s.p1, s.r1, s.l1)
    sum2 = Sum(s.p2, s.r2, s.l2)
    sum3 = Sum(s.p3, s.r3, s.l3)
    s.vsum[...] = jnp.zeros((16, D), F32)

    if NG == 4:
        kv_arrived(peers[1], c, 1)
        kv_send((peers[1], c), 3, peers[2])
        kv_arrived(peers[2], 2 + c, 2)
        kv_send((peers[2], 2 + c), 3, peers[1])
        kv_arrived(peers[1], o, 1)
        kv_send((peers[1], o), 3, peers[2])
        kv_arrived(peers[2], 2 + o, 2)
        kv_send((peers[2], 2 + o), 3, peers[1])
        wo_line.step(0, 2)
        kv_arrived(peers[1], 2 + c, 1)
        kv_arrived(peers[1], 2 + o, 1)
        attend(peers[1])
        kv_arrived(peers[2], c, 2)
        kv_arrived(peers[2], o, 2)
        attend(peers[2])
        wo_line.step(0, 3)
        for j in (c, 2 + c, o, 2 + o):
            kv_arrived(peers[3], j, 3)
        attend(peers[3])
    else:
        for t in range(1, NG):
            arrived(s.kv.at[sources[t]], skv + t)

        def rest(t, _):
            attend(lax.rem(g + t, NG))
            return 0

        lax.fori_loop(1, NG, rest, 0)
        wo_line.step(0, 2)
        wo_line.step(0, 3)

    low = lax.broadcasted_iota(jnp.int32, (256, 128), 1) < HEAD
    thirds = []
    for half in range(2):
        rows = pl.ds(256 * half, 256)
        outs = []
        for h in range(nh):
            outs.append(jnp.transpose(s.acc[2 * h + half] / s.l[2 * h + half]))
            s.attp[h, rows, :] = outs[h].astype(BF)
            s.m[2 * h + half] = s.m[2 * h + half] + jnp.log(s.l[2 * h + half])
        pair = jnp.where(low, roll64(outs[0]), outs[1]).astype(BF)
        s.ab[z, rows, :] = pair
        s.attn[rows, 0:128] = pair
        turned = roll64(outs[2])
        s.attn[rows, 128:256] = jnp.where(low, turned, 0.0).astype(BF)
        thirds.append((turned, outs[2]))
    s.ab[z, 512:768, :] = jnp.where(low, thirds[0][0], thirds[1][1]).astype(BF)
    ab_line = Line(lambda i, u: s.ab.at[i, pl.ds(384 * u, 384)], 2)
    ab_line.start(0)
    ab_line.start(1)

    for t in range(1, T):
        arrived(s.wo.at[lax.rem(z + t, T), o], swo + lax.rem(z + t, T))
    zeros = jnp.zeros((HEAD, D), BF)
    for t in range(T):
        third = s.wo[t].reshape(nh * HEAD, D)[128:192]
        s.wolo[t, 0:HEAD, :] = third
        s.wolo[t, HEAD:BLK, :] = zeros
        s.wohi[t, 0:HEAD, :] = zeros
        s.wohi[t, HEAD:BLK, :] = third
    for k in range(1, T):
        ab_line.step(0, k)
        ab_line.step(1, k)

    left = jnp.concatenate([s.ab[t, 0:512, :] for t in range(T)], axis=1)
    pairs = jnp.concatenate([s.wo[t].reshape(nh * HEAD, D)[0:128] for t in range(T)], axis=0)
    tail = jnp.concatenate([s.ab[t, 512:768, :] for t in range(T)], axis=1)
    g2 = g2_ref[...].reshape(1, -1)
    b2 = b2_ref[...].reshape(1, -1)
    ob = ob_ref[...].reshape(1, -1)
    fcb = fcb_ref[...].reshape(1, -1)
    pb = pb_ref[...].reshape(1, -1)
    for half in range(2):
        third = s.wolo if half == 0 else s.wohi
        s.pre[256 * half:256 * half + 256, :] = (
            dg(left[256 * half:256 * half + 256], pairs, 1, 0)
            + dg(tail, third[...].reshape(T * 128, D), 1, 0))

    def norm2(i, _):
        j = lax.div(i, 2)
        sub = pl.ds(pl.multiple_of(lax.rem(i, 2) * 64, 64), 64)
        rows = pl.ds(pl.multiple_of(i * 64, 64), 64)
        x = s.x[j, sub, :].astype(F32) + s.pre[rows, :] + ob
        s.hid[j, sub, :] = x
        n, _inv = normed(x)
        s.act2[rows, :] = (n * g2 + b2).astype(BF)
        return 0

    lax.fori_loop(0, 8, norm2, 0)

    loads["fc"].wait()
    bias_sum = jnp.zeros((8, F), F32)
    first = jnp.where(z < T // 2, 1, 0)
    for turn in range(2):
        half = first if turn == 0 else 1 - first
        base = pl.multiple_of(half * 256, 256)
        part = pl.ds(base, 256)
        s.pre[part, :] = dg(s.act2[part, :], s.fc[...], 1, 0)

        def gelu(i, total, base=base):
            rows = pl.ds(pl.multiple_of(base + i * 32, 32), 32)
            v = s.pre[rows, :] + fcb
            square = v * v
            th = jnp.tanh(C0 * (v + C1 * square * v))
            one = 1.0 + th
            s.actd[rows, :] = (0.5 * v * one).astype(BF)
            slope = 0.5 * one + (0.5 * v) * (1.0 - th * th) * (C0 * (1.0 + 3.0 * C1 * square))
            grad = slope * s.ga[rows, :]
            s.gpre[rows, :] = grad.astype(BF)
            return total + fold8(grad)

        bias_sum = lax.fori_loop(0, 8, gelu, bias_sum)
        back = dg(s.gpre[part, :], s.fc[...], 1, 1)
        s.p1[2 * half] = back[0:128].astype(BF)
        s.p1[2 * half + 1] = back[128:256].astype(BF)
        if turn == 0:
            sum1.begin(0, (3, 2))
    sum1.begin(0, (1,))
    for u in range(1, U):
        sum1.begin(u, (3, 2, 1))
    s.vsum[8:9, :] = jnp.sum(bias_sum, axis=0, keepdims=True)

    sw1 = new(2 + 2 * NG)

    def weight(dst, index, lhs, rhs):
        for i in range(3):
            part = dg(lhs[:, 256 * i:256 * i + 256], rhs, 0, 0).astype(BF)
            lo, hi = 256 * i, 256 * i + 256
            for qd in range(NG):
                a, b = max(lo, qd * Q1), min(hi, qd * Q1 + Q1)
                if a < b:
                    dst[index, qd, a - qd * Q1:b - qd * Q1, :] = part[a - lo:b - lo]

    def add_into(buf, index, extra):
        def body(i, _):
            buf[index, i] = (buf[index, i].astype(F32) + extra[i].astype(F32)).astype(BF)
            return 0

        lax.fori_loop(0, NG, body, 0)

    weight(s.w1, 0, s.actd, s.cot[...].reshape(N, D))
    weight(s.w1, 1, s.act2, s.gpre[...])
    send(s.w1.at[o], s.w1r, sw1, (mate, z))
    sum1.hop1(0)
    for half in range(2):
        base = 256 * half
        fwd = dg(s.actd[base:base + 256, :], s.pw[...], 1, 0)
        s.p2[2 * half] = fwd[0:128].astype(BF)
        s.p2[2 * half + 1] = fwd[128:256].astype(BF)
    sum1.hop2(0)
    arrived(s.w1r, sw1)
    add_into(s.w1, c, s.w1r)
    for t in range(1, NG):
        send(s.w1.at[c, peers[t]], s.w1s.at[t], sw1 + t, (2 * peers[t] + c, z))

    def back2(u):
        sums = [jnp.zeros((8, D), F32)] * 4
        for i in range(RU // 32):
            rows = pl.ds(RU * u + 32 * i, 32)
            n, inv = normed(s.hid[z, rows, :])
            grad = sum1.total(rows)
            up = s.cot[z, rows, :].astype(F32)
            qg = grad * g2
            gh = up + inv * (qg - jnp.mean(qg, axis=-1, keepdims=True)
                             - n * jnp.mean(qg * n, axis=-1, keepdims=True))
            s.gh[rows, :] = gh
            s.h[z, rows, :] = gh.astype(BF)
            for k, part in enumerate((grad * n, grad, gh, up)):
                sums[k] = sums[k] + fold8(part)
        for k in range(4):
            s.vsum[2 + k:3 + k, :] += jnp.sum(sums[k], axis=0, keepdims=True)

    h_line = Line(pieces_of(s.h), U)
    sum1.last(0)
    back2(0)
    h_line.start(0)
    sum1.hop1(1)
    sum1.hop2(1)
    h_line.step(0, 1)
    sum1.last(1)
    back2(1)
    h_line.start(1)
    sum2.begin(0, (3, 2, 1))
    h_line.step(0, 2)
    h_line.step(1, 1)
    h_line.step(0, 3)
    sum2.begin(1, (3, 2, 1))
    h_line.step(1, 2)
    h_line.step(1, 3)

    grads = dg(s.h[...].reshape(N, D), s.wopad[...], 1, 1)
    for h in range(nh):
        s.do[h] = grads[:, 128 * h:128 * h + 128].astype(BF)
    for h in range(nh):
        for half in range(2):
            rows = pl.ds(256 * half, 256)
            both = s.do[h, rows, :].astype(F32) * s.attp[h, rows, :].astype(F32)
            s.delta[2 * h + half] = jnp.sum(jnp.transpose(both), axis=0, keepdims=True)
    for i in range(2 * nh):
        s.acc[i] = jnp.zeros((128, 256), F32)

    def attend_back(src):
        masks(src)
        for h in range(nh):
            klo, khi = keys_of(src, h)

            def tile(k, half, mask):
                qs = s.q[h, 256 * half:256 * half + 256, :]
                ds_ = s.do[h, 256 * half:256 * half + 256, :]
                sc = dg(k, qs, 1, 1)
                if mask is not None:
                    sc = sc + mask[...]
                p = jnp.exp(sc - s.m[2 * h + half])
                d = p * (dg(k, ds_, 1, 1) - s.delta[2 * h + half])
                p = p.astype(BF)
                d = d.astype(BF)
                return d, dg(d, qs, 1, 0) + dg(p, ds_, 1, 0)

            d1, k1 = tile(klo, 0, s.mlo)
            s.acc[2 * h] += dg(klo, d1, 0, 0)
            d2, k2 = tile(klo, 1, None)
            s.dk[src, h, 0:256, :] = (k1 + k2).astype(BF)
            d3, k3 = tile(khi, 1, s.mhi)
            s.dk[src, h, 256:512, :] = k3.astype(BF)
            s.acc[2 * h + 1] += dg(klo, d2, 0, 0) + dg(khi, d3, 0, 0)

    sdk = new(NG + 2)

    def w1_gather():
        for t in range(1, NG):
            arrived(s.w1s.at[t], sw1 + t)

        def body(i, _):
            rows = pl.ds(pl.multiple_of(i * (Q1 // 3), Q1 // 3), Q1 // 3)
            total = s.w1[c, g, rows, :].astype(F32)
            for t in range(1, NG):
                total = total + s.w1s[t, rows, :].astype(F32)
            s.w1f[c, g, rows, :] = total.astype(BF)
            return 0

        lax.fori_loop(0, 3, body, 0)
        for t in range(1, NG):
            send(s.w1f.at[c, g], s.w1f.at[c, g], sw1 + NG + t, (2 * peers[t] + c, z))

    hand_o = Hand(s.yo, s.mo)
    o_line = Line(pieces_of(s.yo), U, hand_o)

    def finish_output(u):
        for i in range(RU // 32):
            rows = pl.ds(RU * u + 32 * i, 32)
            s.yo[z, rows, :] = (s.hid[z, rows, :] + sum2.total(rows) + pb).astype(BF)
        o_line.start(u)

    half_a = pl.ds(0, 256)
    half_b = pl.ds(256, 256)
    sum2.hop1(0)
    if NG == 4:
        attend_back(peers[3])
        send(s.dk.at[peers[3], :, half_a], s.dka.at[0], sdk + 0, (2 * peers[1] + c, z))
        send(s.dk.at[peers[3], :, half_b], s.dka.at[1], sdk + NG, (2 * peers[2] + c, z))
        attend_back(peers[1])
        w1_gather()
        sum2.hop1(1)
        sum2.hop2(0)
        attend_back(peers[2])
        arrived(s.dka.at[0], sdk + 0)
        for h in range(nh):
            s.dk[peers[2], h, half_a, :] = (s.dk[peers[2], h, half_a, :].astype(F32)
                                            + s.dka[0, h].astype(F32)).astype(BF)
        send(s.dk.at[peers[2]], s.dkr.at[2], sdk + 2, (2 * peers[2] + c, z))
        arrived(s.dka.at[1], sdk + NG)
        for h in range(nh):
            s.dk[peers[1], h, half_b, :] = (s.dk[peers[1], h, half_b, :].astype(F32)
                                            + s.dka[1, h].astype(F32)).astype(BF)
        send(s.dk.at[peers[1]], s.dkr.at[1], sdk + 1, (2 * peers[1] + c, z))
        attend_back(g)
    else:
        def rest_back(t, _):
            attend_back(lax.rem(g + t, NG))
            return 0

        lax.fori_loop(0, NG, rest_back, 0)
        for t in range(1, NG):
            send(s.dk.at[peers[t]], s.dkr.at[t], sdk + t, (2 * peers[t] + c, z))
        w1_gather()
        sum2.hop1(1)
        sum2.hop2(0)
    sum2.hop2(1)
    sum2.last(0)
    finish_output(0)

    sw2 = new(2 + 2 * NG)

    def put2(first, value, rows):
        done = 0
        while done < rows:
            at, off = divmod(first + done, Q2)
            n = min(Q2 - off, rows - done)
            s.w2[at // NG, at % NG, off:off + n, :] = value[done:done + n].astype(BF)
            done += n

    gout = dg(s.attn[...], s.h[...].reshape(N, D), 0, 0)
    put2(3 * nh * HEAD, gout, nh * HEAD)
    sum2.last(1)
    finish_output(1)
    o_line.step(0, 1)
    o_line.step(1, 1)

    got = [1, 2] if NG == 4 else list(range(1, NG))
    for t in got:
        arrived(s.dkr.at[t], sdk + t)
    col = [jnp.zeros((1, 128), F32) for _ in range(5)]
    for half in range(2):
        rows = pl.ds(256 * half, 256)
        dq = [jnp.transpose(s.acc[2 * h + half]) * 0.125 for h in range(nh)]
        dkv = []
        for h in range(nh):
            total = s.dk[g, h, rows, :].astype(F32)
            for t in got:
                total = total + s.dkr[t, h, rows, :].astype(F32)
            dkv.append(total)
        tiles = [
            jnp.where(low, dq[0], roll64(dq[1])),
            jnp.where(low, dq[2], roll64(dkv[0])),
            jnp.where(low, dkv[1], roll64(dkv[2])),
            jnp.where(low, roll64(dkv[0]), dkv[1]),
            jnp.where(low, roll64(dkv[2]), 0.0),
        ]
        for j in range(5):
            col[j] = col[j] + jnp.sum(tiles[j], axis=0, keepdims=True)
            s.gn[rows, 128 * j:128 * j + 128] = tiles[j].astype(BF)
    for turn in range(2):
        half = first if turn == 0 else 1 - first
        part = pl.ds(pl.multiple_of(half * 256, 256), 256)
        back = dg(s.gn[part, :], s.wqt[...], 1, 0)
        s.p3[2 * half] = back[0:128].astype(BF)
        s.p3[2 * half + 1] = back[128:256].astype(BF)
        if turn == 0:
            sum3.begin(0, (3, 2))
    sum3.begin(0, (1,))
    for u in range(1, U):
        sum3.begin(u, (3, 2, 1))
    for j in range(5):
        s.vsum[9:10, 128 * j:128 * j + 128] = col[j]

    act1 = s.act1[...].reshape(N, D)
    for j in range(5):
        n = min(128, 3 * nh * HEAD - 128 * j)
        put2(128 * j, dg(s.gn[:, 128 * j:128 * j + 128], act1, 0, 0), n)
    send(s.w2.at[o], s.w2r, sw2, (mate, z))
    sum3.hop1(0)
    o_line.step(0, 2)
    arrived(s.w2r, sw2)
    add_into(s.w2, c, s.w2r)
    for t in range(1, NG):
        send(s.w2.at[c, peers[t]], s.w2s.at[t], sw2 + t, (2 * peers[t] + c, z))
    sum3.hop2(0)
    o_line.step(1, 2)
    o_line.step(0, 3)

    def back1(u):
        sums = [jnp.zeros((8, D), F32)] * 2
        for i in range(RU // 32):
            rows = pl.ds(RU * u + 32 * i, 32)
            n, inv = normed(s.x[z, rows, :].astype(F32))
            grad = sum3.total(rows)
            qg = grad * g1
            gx = s.gh[rows, :] + inv * (qg - jnp.mean(qg, axis=-1, keepdims=True)
                                        - n * jnp.mean(qg * n, axis=-1, keepdims=True))
            s.yg[z, rows, :] = gx.astype(BF)
            for k, part in enumerate((grad * n, grad)):
                sums[k] = sums[k] + fold8(part)
        for k in range(2):
            s.vsum[k:k + 1, :] += jnp.sum(sums[k], axis=0, keepdims=True)

    hand_g = Hand(s.yg, s.mg)
    y_line = Line(pieces_of(s.yg), U, hand_g)
    v_line = Line(lambda i, u: s.vz.at[i], 1)
    sum3.last(0)
    back1(0)
    y_line.start(0)
    sum3.hop1(1)
    sum3.hop2(1)
    o_line.step(1, 3)
    for t in range(1, NG):
        arrived(s.w2s.at[t], sw2 + t)
    total = s.w2[c, g].astype(F32)
    for t in range(1, NG):
        total = total + s.w2s[t].astype(F32)
    s.w2f[c, g] = total.astype(BF)
    for t in range(1, NG):
        send(s.w2f.at[c, g], s.w2f.at[c, g], sw2 + NG + t, (2 * peers[t] + c, z))
    y_line.step(0, 1)
    sum3.last(1)
    back1(1)
    s.vz[z] = s.vsum[...].astype(BF)
    v_line.start(0)
    y_line.start(1)
    for t in range(1, NG):
        arrived(s.w1f.at[c, sources[t]], sw1 + NG + t)
    send(s.w1f.at[c], s.w1f.at[c], sw1 + 2 * NG, (mate, z))
    hand_o.wait()
    copies = []

    def give(src, dst):
        copy = pltpu.make_async_copy(src, dst, s.ls.at[6 + len(copies)])
        copy.start()
        copies.append(copy)

    for k in range(2):
        give(s.yo.at[2 * k + c], fo_out.at[k, c])
        give(s.mo.at[k], fo_out.at[k, o])
    v_line.step(0, 1)
    y_line.step(0, 2)
    y_line.step(1, 1)
    v_line.step(0, 2)
    arrived(s.w1f.at[o], sw1 + 2 * NG)
    give(s.w1f, w1_out)
    y_line.step(0, 3)
    v_line.step(0, 3)

    svc = new(R)
    upper = s.vz[0, 0:8, :].astype(F32)
    for t in range(1, T):
        upper = upper + s.vz[t, 0:8, :].astype(F32)
    s.vc[r] = jnp.concatenate([upper, s.vsum[8:16, :]], axis=0).astype(BF)
    for t in range(1, R):
        send(s.vc.at[r], s.vc.at[r], svc + t, (lax.rem(r + t, R), z))
    y_line.step(1, 2)
    for t in range(1, NG):
        arrived(s.w2f.at[c, sources[t]], sw2 + NG + t)
    send(s.w2f.at[c], s.w2f.at[c], sw2 + 2 * NG, (mate, z))
    for t in range(1, R):
        arrived(s.vc.at[lax.rem(r + R - t, R)], svc + t)
    total = s.vc[0].astype(F32)
    for t in range(1, R):
        total = total + s.vc[t].astype(F32)
    s.vsum[...] = total
    give(s.vsum, v_out)
    arrived(s.w2f.at[o], sw2 + 2 * NG)
    give(s.w2f, w2_out)
    y_line.step(1, 3)
    hand_g.wait()
    for k in range(2):
        give(s.yg.at[2 * k + c], fg_out.at[k, c])
        give(s.mg.at[k], fg_out.at[k, o])
    for cond, done in pending:
        if cond is None:
            done()
        else:
            pl.when(cond)(done)
    for copy in copies:
        copy.wait()


def finish_kernel(R, NS, pos_ref, seq_ref, rank_ref, w1_ref, w2_ref, fo_ref, fg_ref, v_ref, out_ref, gt_ref,
                  ln1g_ref, ln1b_ref, gq_ref, gqv_ref, go_ref, ob_ref, ln2g_ref, ln2b_ref, gf_ref, fb_ref,
                  gp_ref, pb_ref):
    i = pl.program_id(0)
    gp_ref[...] = w1_ref[0].astype(F32)
    gf_ref[...] = w1_ref[1].astype(F32)

    @pl.when(i < 6)
    def _():
        gq_ref[...] = w2_ref[...].astype(F32)

    @pl.when(i >= 6)
    def _():
        go_ref[...] = w2_ref[...].astype(F32)

    @pl.when(i < 4)
    def _():
        b = 4 * rank_ref[0] + i
        high = jnp.where(pos_ref[b] < R, 0, 1)
        out_ref[...] = fo_ref[high, seq_ref[b]]
        gt_ref[...] = fg_ref[high, seq_ref[b]]

    @pl.when(i == 0)
    def _():
        for ref, k in ((ln1g_ref, 0), (ln1b_ref, 1), (ln2g_ref, 2), (ln2b_ref, 3), (ob_ref, 4), (pb_ref, 5),
                       (fb_ref, 8)):
            ref[...] = v_ref[k:k + 1, :].reshape(-1)
        gqv_ref[0:1, :] = v_ref[9:10, 0:192]
        gqv_ref[1:2, :] = v_ref[9:10, 384:576]


def per_device(R, T, tokens, cotangent, block_pos, block_seq, ln1_gain, ln1_bias, qkv_weight, qv_bias,
               out_weight, out_bias, ln2_gain, ln2_bias, fc_weight, fc_bias, proj_weight, proj_bias):
    D = tokens.shape[1]
    F = fc_weight.shape[1]
    local = qkv_weight.shape[2]
    nh = local // HEAD
    NG = R // 2
    sizes = scratch_list(R, T, D, F, nh)
    names = [n for n, _ in sizes]
    row = lambda v: v
    wqt = jnp.transpose(qkv_weight, (1, 2, 0)).reshape(3 * local, D)
    sm = pl.BlockSpec(memory_space=pltpu.SMEM)
    vm = pl.BlockSpec(memory_space=pltpu.VMEM)
    hb = pl.BlockSpec(memory_space=pl.ANY)
    w1, w2, fo, fg, vs = pl.pallas_call(
        functools.partial(layer_kernel, R, T, D, F, nh, names),
        out_shape=(
            jax.ShapeDtypeStruct((2, NG, D // NG, D), BF),
            jax.ShapeDtypeStruct((2, NG, D // 2 // NG, D), BF),
            jax.ShapeDtypeStruct((2, 2, BLK, D), BF),
            jax.ShapeDtypeStruct((2, 2, BLK, D), BF),
            jax.ShapeDtypeStruct((16, D), F32),
        ),
        in_specs=[sm, sm, hb, hb, vm, vm, hb, vm, hb, vm, vm, vm, hb, vm, hb, vm],
        out_specs=(hb, hb, hb, hb, hb),
        scratch_shapes=[sp for _, sp in sizes],
        compiler_params=pltpu.CompilerParams(
            collective_id=0, has_side_effects=True, vmem_limit_bytes=67043328),
        name="layer",
    )(block_pos, block_seq, tokens.reshape(4, BLK, D), cotangent.reshape(4, BLK, D), row(ln1_gain),
      row(ln1_bias), wqt, qv_bias, out_weight.reshape(2, local // 2, D), row(out_bias), row(ln2_gain), row(ln2_bias), fc_weight,
      row(fc_bias), proj_weight, row(proj_bias))

    rank = lax.axis_index("ctx").astype(jnp.int32).reshape(1)
    NS = 8
    rb = D // NS
    whole = lambda *shape: pl.BlockSpec(shape, lambda i: (0,) * len(shape))
    vec = jax.ShapeDtypeStruct((D,), F32)
    outs = pl.pallas_call(
        functools.partial(finish_kernel, R, NS),
        grid=(NS,),
        out_shape=(
            jax.ShapeDtypeStruct((4 * BLK, D), BF),
            jax.ShapeDtypeStruct((4 * BLK, D), BF),
            vec, vec,
            jax.ShapeDtypeStruct((3 * local, D), F32),
            jax.ShapeDtypeStruct((2, local), F32),
            jax.ShapeDtypeStruct((local, D), F32),
            vec, vec, vec,
            jax.ShapeDtypeStruct((D, F), F32),
            vec,
            jax.ShapeDtypeStruct((F, D), F32),
            vec,
        ),
        in_specs=[sm, sm, sm,
                  pl.BlockSpec((2, rb, D), lambda i: (0, i, 0)),
                  pl.BlockSpec((rb, D), lambda i: (i, 0)),
                  whole(2, 2, BLK, D), whole(2, 2, BLK, D), whole(16, D)],
        out_specs=(
            pl.BlockSpec((BLK, D), lambda i: (jnp.minimum(i, 3), 0)),
            pl.BlockSpec((BLK, D), lambda i: (jnp.minimum(i, 3), 0)),
            whole(D), whole(D),
            pl.BlockSpec((rb, D), lambda i: (jnp.minimum(i, 5), 0)),
            whole(2, local),
            pl.BlockSpec((rb, D), lambda i: (jnp.maximum(i - 6, 0), 0)),
            whole(D), whole(D), whole(D),
            pl.BlockSpec((rb, F), lambda i: (i, 0)),
            whole(F),
            pl.BlockSpec((rb, D), lambda i: (i, 0)),
            whole(D),
        ),
        name="finish",
    )(block_pos, block_seq, rank, w1.reshape(2, D, D), w2.reshape(D, D), fo, fg, vs)
    (output, grad_tokens, ln1g, ln1b, gq, gqv, go, ob, ln2g, ln2b, gf, fb, gp, pb) = outs
    flat = lambda v: v
    return (output, grad_tokens, flat(ln1g), flat(ln1b),
            jnp.transpose(gq.reshape(3, local, D), (2, 0, 1)), gqv, go, flat(ob), flat(ln2g), flat(ln2b),
            gf, flat(fb), gp, flat(pb))


def solution(mesh):
    R = mesh.shape["ctx"]
    T = mesh.shape["tp"]
    return jax.shard_map(
        functools.partial(per_device, R, T),
        mesh=mesh,
        in_specs=(
            P("ctx", None), P("ctx", None), P(), P(), P(), P(), P(None, None, "tp"), P(None, "tp"),
            P("tp", None), P(), P(), P(), P(None, "tp"), P("tp"), P("tp", None), P(),
        ),
        out_specs=(
            P("ctx", None), P("ctx", None), P(), P(), P(None, None, "tp"), P(None, "tp"), P("tp", None),
            P(), P(), P(), P(None, "tp"), P("tp"), P("tp", None), P(),
        ),
        check_vma=False,
    )
```

time: 221 us -> 145 us (0.66); the launches traced: 219 us -> 145 us
  Pallas kernels: 200 us -> 144 us
  other arithmetic: 8.96 us -> 0 us
  local copies, waits for them, and re-layouts: 8.87 us -> 0 us
    pallas_call x1, Pallas kernels: 192 us -> 136 us  [per_device(): pl.pallas_call(functools.partial(layer_kernel, R, T, D, F, nh, names), ou...]
    pallas_call x7 -> x0, other arithmetic: 8.96 us -> none  [per_device(): pl.pallas_call(functools.partial(finish_kernel, R, NS), grid=(NS,), out_s...]
    reshape x7 -> x0, local copies, waits for them, and re-layouts: 8.87 us -> none  [per_device(): row = lambda v: v.reshape(1, -1)]
where the time goes in v1:
time: 145 us
  Pallas kernels  144 us (99%)
    pallas_call x1, Pallas kernels, per_device(): pl.pallas_call(functools.partial(layer_kernel, R, T, D, F, nh, names), ou...  136 us
    pallas_call x1, Pallas kernels, per_device(): pl.pallas_call(functools.partial(finish_kernel, R, NS), grid=(NS,), out_s...  8.11 us

profile of v1, /device:TPU:1, one launch (start us, length us, event | category | flops | bytes accessed | tf_op | source)
XLA Modules:
  0.0 144.8 jit_solution(1664389124012129036)
XLA Ops:
  0.7 135.8 %layer.1 = (bf16[2,4,192,768]{3,2,1,0:T(8,128)(2,1)}, bf16[2,4,96,768]{3,2,1,0:T(8,128)(2,1)}, bf16[2,2,128,768]{3,2,1,0:T(8,128)(2,1)}, bf16[2,2,128,768]{3,2,1,0:T(8,128)(2,1)}, f32[16,768]{1,0:T(8,128)}) custom-call(s32[32]{0:T(128)} %pos_ref.1, s32[32]{0:T(128)} %seq_ref.1, bf16[4,128,768]{2,1,0:T(8,128)(2,1)} %bitcast.15, ...), custom_call_target="tpu_custom_call" | custom-call | tf_op jit(solution)/shard_map/layer/pallas_call | solution.py:980
  136.5 8.1 %finish.1 = (bf16[512,768]{1,0:T(8,128)(2,1)}, bf16[512,768]{1,0:T(8,128)(2,1)}, f32[768]{0:T(1024)}, f32[768]{0:T(1024)}, f32[576,768]{1,0:T(8,128)}, /*index=5...) custom-call(s32[32]{0:T(128)} %pos_ref.1, ...), custom_call_target="tpu_custom_call" | custom-call | tf_op jit(solution)/shard_map/finish/pallas_call | solution.py:1004
